TPU v7x, 128 devices: a whole 4x4x4 slice. The times are simulated.
128 devices in a mesh: grp: 4 (over z), tile: 32 (over x, y, core).
Axes of the slice: x: 4, y: 4, z: 4, core: 2. Of those that a mesh axis runs over, the one named last changes fastest.
Arguments:
- noise: bfloat16 [16, 3, 2048, 2048], P('grp', None, 'tile'), may hold values from -6 to 6
- stress: float32 [6, 2048, 2048], P(None, 'tile', 'grp'), as said below
- timescale: float32 [2048, 2048], P('tile', 'grp'), may hold values from 3 to 256
- mean_inflow: float32 [2048, 2048], P('tile', 'grp'), may hold values from 0.5 to 1.5
- courant: float32 [2048, 2048], P('tile', 'grp'), may hold values from 0.2 to 0.9
- prior_state: float32 [3, 2048, 2048], P(None, 'tile', 'grp'), may hold values from -6 to 6
- field: float32 [3, 8, 2048, 2048], P(None, None, 'tile', 'grp'), may hold values from -6 to 6
Outputs:
- inflow: bfloat16 [16, 3, 2048, 2048], P(None, None, 'tile', 'grp')
- field_out: float32 [3, 8, 2048, 2048], P(None, None, 'tile', 'grp')
Inputs may be any that keep to these rules, and one draw needn't show every extreme that they name: stress holds, per cell, R11, R21, R22, R31, R32, R33 of a symmetric positive definite tensor whose Cholesky factor has diagonal entries of 0.3 or more.
All inputs are finite; a program needn't handle non-finite values.
Results may differ from a plain program's by a relative error of at most 0.0085.
Values may be sent and summed in bfloat16 or wider, within the bound.
A program may use at most 128 MiB of HBM per device.

v0:
```python
import math
import jax
import jax.numpy as jnp
from jax import lax
from jax.sharding import PartitionSpec as P

LS = 2
FW = 4


def padded_2(value, sides, width, wrap):
    for axis, dim in sides:
        devices, length = (lax.axis_size(axis), value.shape[dim])
        up = [(i, (i + 1) % devices) for i in range(devices if wrap else devices - 1)]
        down = [(j, i) for i, j in up]
        last = lax.slice_in_dim(value, length - width, length, axis=dim)
        initial = lax.slice_in_dim(value, 0, width, axis=dim)
        before = lax.ppermute(last, axis, up)
        after = lax.ppermute(initial, axis, down)
        value = jnp.concatenate([before, value, after], axis=dim)
    return value


def filter_taps():
    offsets = jnp.arange(-FW, FW + 1).astype(jnp.float32)
    raw = jnp.exp(-math.pi * offsets * offsets / (2.0 * LS * LS))
    return (raw / jnp.sqrt(jnp.sum(raw * raw))).astype(jnp.bfloat16)


def band_matrix(rows, taps):
    width = taps.shape[0]
    distance = jnp.arange(rows + width - 1)[None, :] - jnp.arange(rows)[:, None]
    picks = distance[:, :, None] == jnp.arange(width)[None, None, :]
    return jnp.sum(jnp.where(picks, taps.astype(jnp.float32), 0.0), axis=2).astype(jnp.bfloat16)


def filter_last(padded, taps):
    width = taps.shape[0]
    length = padded.shape[-1] - width + 1
    block = math.gcd(length, 128)
    weights = band_matrix(block, taps)
    windows = jnp.stack(
        [
            lax.slice_in_dim(padded, start, start + block + width - 1, axis=padded.ndim - 1)
            for start in range(0, length, block)
        ],
        axis=-2,
    )
    result = jnp.einsum("...kw,bw->...kb", windows, weights, preferred_element_type=jnp.float32)
    return result.reshape(result.shape[:-2] + (length,))


def filter_rows(padded, taps):
    rows = padded.shape[2] - taps.shape[0] + 1
    weights = band_matrix(rows, taps)
    return jnp.einsum("ij,pcjz->pciz", weights, padded, preferred_element_type=jnp.float32)


def cholesky_cells(stress):
    first_diag = jnp.sqrt(stress[0])
    second_low = stress[1] / first_diag
    second_diag = jnp.sqrt(stress[2] - second_low * second_low)
    third_low = stress[3] / first_diag
    third_mid = (stress[4] - second_low * third_low) / second_diag
    third_diag = jnp.sqrt(stress[5] - third_low * third_low - third_mid * third_mid)
    return (first_diag, second_low, second_diag, third_low, third_mid, third_diag)


def velocity_of(state, factors, mean_inflow):
    first_diag, second_low, second_diag, third_low, third_mid, third_diag = factors
    return jnp.stack(
        [
            mean_inflow + first_diag * state[0],
            second_low * state[0] + second_diag * state[1],
            third_low * state[0] + third_mid * state[1] + third_diag * state[2],
        ]
    )


def march(current, courant, velocity):
    upstream = jnp.concatenate([velocity[:, None], current[:, :-1]], axis=1)
    return (1.0 - courant) * current + courant * upstream


def tile_chain(filtered, stress, timescale, mean_inflow, courant, prior_state, field):
    decay = jnp.exp(-math.pi / (2.0 * timescale))
    gain = jnp.sqrt(1.0 - decay * decay)
    factors = cholesky_cells(stress)

    def advance(carry, plane):
        state, current = carry
        state = decay * state + gain * plane
        velocity = velocity_of(state, factors, mean_inflow)
        return ((state, march(current, courant, velocity)), velocity.astype(jnp.bfloat16))

    (state, result), inflow = lax.scan(advance, (prior_state, field), filtered)
    return (inflow, result)


def body(noise, stress, timescale, mean_inflow, courant, prior_state, field):
    taps = filter_taps()
    flipped = jnp.swapaxes(noise, 2, 3)
    tiles = lax.all_to_all(
        lax.all_to_all(flipped, "tile", split_axis=2, concat_axis=3, tiled=True),
        "grp",
        split_axis=3,
        concat_axis=0,
        tiled=True,
    )
    banded = padded_2(tiles, (("grp", 3),), FW, False)
    widened = padded_2(banded, (("tile", 2),), FW, True)
    span = filter_rows(widened, taps).astype(jnp.bfloat16)
    filtered = filter_last(span, taps)
    inflow, result = tile_chain(
        filtered, stress, timescale, mean_inflow, courant, prior_state, field
    )
    return (inflow, result)


def solution(mesh):
    placed = (
        P("grp", None, "tile", None),
        P(None, "tile", "grp"),
        P("tile", "grp"),
        P("tile", "grp"),
        P("tile", "grp"),
        P(None, "tile", "grp"),
        P(None, None, "tile", "grp"),
    )
    return jax.shard_map(
        body,
        mesh=mesh,
        in_specs=placed,
        out_specs=(P(None, None, "tile", "grp"), P(None, None, "tile", "grp")),
        check_vma=False,
    )
```

profile of v0, /device:TPU:63, one launch (start us, length us, event | category | flops | bytes accessed | tf_op | source)
XLA Modules:
  0.0 310.5 jit_solution(12647594609920412347)
XLA Ops:
  0.6 1.9 copy-done.7
  2.5 7.1 %copy.41 = bf16[4,3,64,2048]{2,0,1,3:T(4,128)(2,1)} copy(bf16[4,3,64,2048]{3,2,1,0:T(8,128)(2,1)S(1)} %copy-done.7) | data formatting | bytes 6291456 | tf_op args[0]
  9.6 7.7 %bitcast_bitcast_fusion = bf16[2048,3,4,64]{3,2,1,0:T(4,128)(2,1)} fusion(bf16[4,3,64,2048]{2,0,1,3:T(4,128)(2,1)} %copy.41), kind=kLoop, calls=%fused_computation.73 | loop fusion | bytes 6291456
  17.3 7.5 %reshape.107 = bf16[32,2,24576]{2,1,0:T(2,128)(2,1)S(1)} reshape(bf16[2048,3,4,64]{3,2,1,0:T(4,128)(2,1)} %bitcast_bitcast_fusion) | data formatting | bytes 6291456
  24.8 43.9 %all_to_all.36 = bf16[32,2,24576]{2,1,0:T(2,128)(2,1)} all-to-all(bf16[32,2,24576]{2,1,0:T(2,128)(2,1)S(1)} %reshape.107), channel_id=1, replica_groups=mesh['grp'=4,'tile'=32] {'tile'}, dimensions={0} | all-to-all | bytes 6291456 | tf_op jit(solution)/shard_map/all_to_all | solution.py:104
  68.7 8.7 %reshape.108 = bf16[2048,3,4,64]{3,2,1,0:T(4,128)(2,1)} reshape(bf16[32,2,24576]{2,1,0:T(2,128)(2,1)} %all_to_all.36) | data formatting | bytes 6291456
  77.4 9.5 %copy.65 = bf16[4,3,32,64,64]{4,2,3,1,0:T(8,128)(2,1)} copy(bf16[4,3,32,64,64]{4,0,1,3,2:T(4,128)(2,1)} %bitcast.127) | data formatting | bytes 6291456 | tf_op jit(solution)/shard_map/all_to_all | solution.py:104
  86.9 11.8 %copy.54 = bf16[4,3,64,32,64]{2,0,1,4,3:T(4,128)(2,1)} copy(bf16[4,3,64,32,64]{4,3,2,1,0:T(8,128)(2,1)} %bitcast.128) | data formatting | bytes 6291456 | tf_op jit(solution)/shard_map/all_to_all | solution.py:104
  98.7 7.7 %reshape.109 = bf16[4,2,196608]{2,1,0:T(2,128)(2,1)} reshape(bf16[2048,3,4,64]{3,2,1,0:T(4,128)(2,1)} %bitcast.129) | data formatting | bytes 6291456
  106.5 5.0 %all-to-all-start.1 = ((bf16[4,2,196608]{2,1,0:T(2,128)(2,1)}), bf16[4,2,196608]{2,1,0:T(2,128)(2,1)S(1)}, u32[]{:S(2)}, u32[]{:S(2)}) async-start(bf16[4,2,196608]{2,1,0:T(2,128)(2,1)} %reshape.109), calls=%async_computation.1 | async-start | bytes 6291456 | tf_op jit(solution)/shard_map/all_to_all | solution.py:103
  112.9 2.2 fusion.24
  117.4 30.1 %all-to-all-done.1 = bf16[4,2,196608]{2,1,0:T(2,128)(2,1)S(1)} async-done(((bf16[4,2,196608]{2,1,0:T(2,128)(2,1)}), bf16[4,2,196608]{2,1,0:T(2,128)(2,1)S(1)}, u32[]{:S(2)}, u32[]{:S(2)}) %all-to-all-start.1) | async-done | bytes 3145760 | tf_op jit(solution)/shard_map/all_to_all | solution.py:103
  147.5 5.3 %reshape.110 = bf16[2048,3,4,64]{3,2,1,0:T(4,128)(2,1)} reshape(bf16[4,2,196608]{2,1,0:T(2,128)(2,1)S(1)} %all-to-all-done.1) | data formatting | bytes 6291456
  152.8 8.3 %copy.45 = bf16[4,4,3,64,512]{4,3,2,1,0:T(8,128)(2,1)S(1)} copy(bf16[4,4,3,64,512]{3,1,2,4,0:T(4,128)(2,1)} %bitcast.130) | data formatting | bytes 6291456 | tf_op jit(solution)/shard_map/all_to_all | solution.py:103
  165.7 3.1 collective-permute-start.1
  168.8 2.4 collective-permute-start
  171.3 2.3 collective-permute-done
  176.1 1.8 pad_maximum_fusion.3
  177.9 5.7 %collective-permute-start.2 = (bf16[16,3,4,520]{3,2,1,0:T(4,128)(2,1)S(1)}, bf16[16,3,4,520]{3,2,1,0:T(4,128)(2,1)S(1)}, u32[]{:S(2)}, u32[]{:S(2)}) collective-permute-start(bf16[16,3,4,520]{3,2,1,0:T(4,128)(2,1)S(1)} %get-tuple-element.126), channel_id=1, source_target_pairs={{0,1},{1,2},{2,3},{3,4},{4,5},{5,6},{6,7},{7,8},{8,9},{9,10},{10,1... | collective-permute-start | bytes 599048 | tf_op jit(solution)/shard_map/ppermute | solution.py:18
  186.7 5.8 %collective-permute-done.3 = bf16[16,3,4,520]{3,2,1,0:T(4,128)(2,1)S(1)} collective-permute-done((bf16[16,3,4,520]{3,2,1,0:T(4,128)(2,1)S(1)}, bf16[16,3,4,520]{3,2,1,0:T(4,128)(2,1)S(1)}, u32[]{:S(2)}, u32[]{:S(2)}) %collective-permute-start.3) | collective-permute-done | bytes 199712 | tf_op jit(solution)/shard_map/ppermute | solution.py:19
  192.5 4.2 %convert_bitcast_fusion.3 = bf16[16,3,64,520]{3,2,1,0:T(8,128)(2,1)S(1)} fusion(bf16[16,3,4,520]{3,2,1,0:T(4,128)(2,1)S(1)} %collective-permute-done.3, bf16[16,3,64,4]{3,2,1,0:T(8,128)(2,1)S(1)} %copy-done.6, bf16[16,3,64,512]{3,2,1,0:T(8,128)(2,1)S(1)} %bitcast.133, bf16[16,3,64,4]{3,2,1,0:T(8,128)(2,1)S(1)} %copy-done.5, ...), kind=kOutput, calls=%fused_computation.35 | convolution fusion | flops 249600000 | bytes 6798336 | tf_op jit(solution)/shard_map/ij,pcjz->pciz/dot_general | solution.py:56
  197.6 2.6 fusion.18
  200.2 3.5 %copy.64 = f32[16,3,4,8,8,128]{5,4,2,3,1,0:T(8,128)} copy(f32[16,3,4,8,8,128]{5,4,3,2,1,0:T(8,128)S(1)} %fusion.18) | data formatting | bytes 12582912 | tf_op jit(solution)/shard_map/reshape | solution.py:50
  203.7 105.1 %while.14 = (s32[]{:T(128)}, f32[3,64,512]{2,1,0:T(8,128)S(1)}, f32[3,8,64,512]{3,2,1,0:T(8,128)S(1)}, bf16[16,3,64,512]{3,2,1,0:T(8,128)(2,1)}, f32[64,512]{1,0...) while((s32[]{:T(128)}, f32[3,64,512]{2,1,0:T(8,128)S(1)}, ...), condition=%wide.region_4.5_spmd, body=%wide.region_3.4_spmd.sunk | while | flops 4685826 | bytes 20512960 | solution.py:96
  (177 shorter events, 120.6 us)
Async XLA Ops:
  0.6 1.9 copy-start.7
  106.5 6.5 %copy-start.8 = (f32[64,512]{1,0:T(8,128)S(1)}, f32[64,512]{1,0:T(8,128)}, u32[]{:S(2)}) copy-start(f32[64,512]{1,0:T(8,128)} %param.11) | copy-start | bytes 393220
  106.5 41.0 %all-to-all-start.1 = ((bf16[4,2,196608]{2,1,0:T(2,128)(2,1)}), bf16[4,2,196608]{2,1,0:T(2,128)(2,1)S(1)}, u32[]{:S(2)}, u32[]{:S(2)}) async-start(bf16[4,2,196608]{2,1,0:T(2,128)(2,1)} %reshape.109), calls=%async_computation.1 | async-start | bytes 6291456 | tf_op jit(solution)/shard_map/all_to_all | solution.py:103
  165.7 9.2 %collective-permute-start.1 = (bf16[16,3,64,4]{2,0,3,1:T(8,128)(2,1)S(1)}, bf16[16,3,64,4]{2,0,3,1:T(8,128)(2,1)S(1)}, u32[]{:S(2)}, u32[]{:S(2)}) collective-permute-start(bf16[16,3,64,4]{2,0,3,1:T(8,128)(2,1)S(1)} %copy.47), channel_id=1, source_target_pairs={{32,0},{64,32},{96,64},{33,1},{65,33},{97,65},{34,2},{66,34},{98,6... | collective-permute-start | bytes 73736 | tf_op jit(solution)/shard_map/ppermute | solution.py:19
  168.8 4.8 %collective-permute-start = (bf16[16,3,64,4]{2,0,3,1:T(8,128)(2,1)S(1)}, bf16[16,3,64,4]{2,0,3,1:T(8,128)(2,1)S(1)}, u32[]{:S(2)}, u32[]{:S(2)}) collective-permute-start(bf16[16,3,64,4]{2,0,3,1:T(8,128)(2,1)S(1)} %copy.46), channel_id=1, source_target_pairs={{0,32},{32,64},{64,96},{1,33},{33,65},{65,97},{2,34},{34,66},{66,9... | collective-permute-start | bytes 73736 | tf_op jit(solution)/shard_map/ppermute | solution.py:18
  176.1 16.4 %copy-start.5 = (bf16[16,3,64,4]{3,2,1,0:T(8,128)(2,1)S(1)}, bf16[16,3,64,4]{3,2,1,0:T(8,128)(2,1)}, u32[]{:S(2)}) copy-start(bf16[16,3,64,4]{3,2,1,0:T(8,128)(2,1)} %copy.48) | copy-start | bytes 73732
  176.1 16.4 %copy-start.6 = (bf16[16,3,64,4]{3,2,1,0:T(8,128)(2,1)S(1)}, bf16[16,3,64,4]{3,2,1,0:T(8,128)(2,1)}, u32[]{:S(2)}) copy-start(bf16[16,3,64,4]{3,2,1,0:T(8,128)(2,1)} %copy.49) | copy-start | bytes 73732
  177.9 8.8 %collective-permute-start.2 = (bf16[16,3,4,520]{3,2,1,0:T(4,128)(2,1)S(1)}, bf16[16,3,4,520]{3,2,1,0:T(4,128)(2,1)S(1)}, u32[]{:S(2)}, u32[]{:S(2)}) collective-permute-start(bf16[16,3,4,520]{3,2,1,0:T(4,128)(2,1)S(1)} %get-tuple-element.126), channel_id=1, source_target_pairs={{0,1},{1,2},{2,3},{3,4},{4,5},{5,6},{6,7},{7,8},{8,9},{9,10},{10,1... | collective-permute-start | bytes 599048 | tf_op jit(solution)/shard_map/ppermute | solution.py:18
  183.6 8.9 %collective-permute-start.3 = (bf16[16,3,4,520]{3,2,1,0:T(4,128)(2,1)S(1)}, bf16[16,3,4,520]{3,2,1,0:T(4,128)(2,1)S(1)}, u32[]{:S(2)}, u32[]{:S(2)}) collective-permute-start(bf16[16,3,4,520]{3,2,1,0:T(4,128)(2,1)S(1)} %get-tuple-element.127), channel_id=1, source_target_pairs={{1,0},{2,1},{3,2},{4,3},{5,4},{6,5},{7,6},{8,7},{9,8},{10,9},{11,1... | collective-permute-start | bytes 599048 | tf_op jit(solution)/shard_map/ppermute | solution.py:19
  200.2 3.5 %copy-start.1 = (f32[3,8,64,512]{3,2,1,0:T(8,128)S(1)}, f32[3,8,64,512]{3,2,1,0:T(8,128)}, u32[]{:S(2)}) copy-start(f32[3,8,64,512]{3,2,1,0:T(8,128)} %param.15) | copy-start | bytes 9437188
  200.2 3.5 %copy-start.2 = (f32[3,64,512]{2,1,0:T(8,128)S(1)}, f32[3,64,512]{2,1,0:T(8,128)}, u32[]{:S(2)}) copy-start(f32[3,64,512]{2,1,0:T(8,128)} %param.14) | copy-start | bytes 1179652
  207.3 0.9 copy-start.3
  213.8 0.9 copy-start.3
  220.4 0.9 copy-start.3
  227.0 0.9 copy-start.3
  233.6 0.9 copy-start.3
  240.1 0.9 copy-start.3
  246.7 0.9 copy-start.3
  253.3 0.9 copy-start.3
  259.8 0.9 copy-start.3
  266.4 0.9 copy-start.3
  273.0 0.9 copy-start.3
  279.5 0.9 copy-start.3
  308.8 1.7 copy-start
  (5 other events, 4.3 us)
where the time goes:
time: 313 us; the launch traced here: 310 us
  local copies, waits for them, and re-layouts  105 us (34%)
  other arithmetic  97.3 us (31%)
  blocking collectives  43.9 us (14%)
  waiting for transfers between devices  39.8 us (13%)
  starting transfers between devices  16.1 us (5%)
  matrix products  6.73 us (2%)
    unnamed x22, local copies, waits for them, and re-layouts  48.3 us
    all_to_all x1, blocking collectives, body(): lax.all_to_all(flipped, 'tile', split_axis=2, concat_axis=3, tiled=True)  43.9 us
    all_to_all x1, waiting for transfers between devices, body(): lax.all_to_all(lax.all_to_all(flipped, 'tile', split_axis=2, concat_axis=...  30.1 us
    another operation x16, other arithmetic, velocity_of(): jnp.stack([mean_inflow + first_diag * state[0], second_low * state[0] + s...  22.1 us
    add x16, other arithmetic, march(): return (1.0 - courant) * current + courant * upstream  22.1 us
    all_to_all x2, local copies, waits for them, and re-layouts, body(): lax.all_to_all(flipped, 'tile', split_axis=2, concat_axis=3, tiled=True)  21.3 us
    add x16, other arithmetic, advance(): state = decay * state + gain * plane  20.4 us
    sub x16, other arithmetic, march(): return (1.0 - courant) * current + courant * upstream  14.6 us
  transfers between devices with their start and end apart: 5, of which 4 were waited for; matrix products, arithmetic and copies ran while one was open for 2% of the time, Pallas kernels for 0%

commit v1 on v0

--- a/solution.py
+++ b/solution.py
@@ -6,6 +6,29 @@
 
 LS = 2
 FW = 4
+
+
+def split_up(array, dim, size):
+    shape = array.shape
+    blocks = array.reshape(*shape[:dim], size, shape[dim] // size, *shape[dim + 1 :])
+    return jnp.moveaxis(blocks, dim, 0)
+
+
+def in_order(blocks, dim):
+    shape = list(blocks.shape[1:])
+    shape[dim] *= blocks.shape[0]
+    return jnp.moveaxis(blocks, 0, dim).reshape(shape)
+
+
+def sent_to_each(value, axis, split_dim, concat_dim):
+    size, place = (lax.axis_size(axis), lax.axis_index(axis))
+    pieces = split_up(value, split_dim, size)
+    done = [pieces[place]]
+    for step in range(1, size):
+        sent = pieces[(place + step) % size]
+        done.append(lax.ppermute(sent, axis, [(i, (i + step) % size) for i in range(size)]))
+    pieces = jnp.stack(done)[(place - jnp.arange(size)) % size]
+    return in_order(pieces, concat_dim)
 
 
 def padded_2(value, sides, width, wrap):
@@ -100,12 +123,8 @@
 def body(noise, stress, timescale, mean_inflow, courant, prior_state, field):
     taps = filter_taps()
     flipped = jnp.swapaxes(noise, 2, 3)
-    tiles = lax.all_to_all(
-        lax.all_to_all(flipped, "tile", split_axis=2, concat_axis=3, tiled=True),
-        "grp",
-        split_axis=3,
-        concat_axis=0,
-        tiled=True,
+    tiles = sent_to_each(
+        lax.all_to_all(flipped, "tile", split_axis=2, concat_axis=3, tiled=True), "grp", 3, 0
     )
     banded = padded_2(tiles, (("grp", 3),), FW, False)
     widened = padded_2(banded, (("tile", 2),), FW, True)

time: 313 us -> 296 us (0.946)
  blocking collectives: 43.9 us -> 0 us
  waiting for transfers between devices: 39.8 us -> 75 us
  local copies, waits for them, and re-layouts: 105 us -> 89.3 us
  starting transfers between devices: 16.1 us -> 23.7 us
    all_to_all x1 -> x0, blocking collectives: 43.9 us -> none  [body(): lax.all_to_all(flipped, 'tile', split_axis=2, concat_axis=3, tiled=True)]
    ppermute x0 -> x3, waiting for transfers between devices: none -> 31.2 us  [sent_to_each(): lax.ppermute(sent, axis, [(i, (i + step) % size) for i in range(size)])]
    unnamed x22 -> x26, local copies, waits for them, and re-layouts: 48.3 us -> 35 us
    all_to_all x2 -> x1, local copies, waits for them, and re-layouts: 21.3 us -> 9.46 us  [body(): lax.all_to_all(flipped, 'tile', split_axis=2, concat_axis=3, tiled=True)]
    reshape x0 -> x1, local copies, waits for them, and re-layouts: none -> 8.47 us  [split_up(): array.reshape(*shape[:dim], size, shape[dim] // size, *shape[dim + 1:])]
    all_to_all x1 -> x0, local copies, waits for them, and re-layouts: 8.27 us -> none  [body(): lax.all_to_all(lax.all_to_all(flipped, 'tile', split_axis=2, concat_axis=...]
    another operation x0 -> x1, local copies, waits for them, and re-layouts: none -> 7.01 us
    all_to_all x1, waiting for transfers between devices: 30.1 us -> 35 us  [body(): lax.all_to_all(flipped, 'tile', split_axis=2, concat_axis=3, tiled=True)]
  transfers between devices with their start and end apart: 5 -> 8, of which waited for: 4 -> 7; matrix products, arithmetic and copies ran while one was open for 2% -> 2% of each run, Pallas kernels for 0% -> 0%
where the time goes in v1:
time: 296 us; the launch traced here: 294 us
  other arithmetic  97.1 us (33%)
  local copies, waits for them, and re-layouts  89.3 us (30%)
  waiting for transfers between devices  75 us (25%)
  starting transfers between devices  23.7 us (8%)
  matrix products  6.74 us (2%)
    all_to_all x1, waiting for transfers between devices, body(): lax.all_to_all(flipped, 'tile', split_axis=2, concat_axis=3, tiled=True)  35 us
    unnamed x26, local copies, waits for them, and re-layouts  35 us
    ppermute x3, waiting for transfers between devices, sent_to_each(): lax.ppermute(sent, axis, [(i, (i + step) % size) for i in range(size)])  31.2 us
    another operation x16, other arithmetic, velocity_of(): jnp.stack([mean_inflow + first_diag * state[0], second_low * state[0] + s...  22.1 us
    add x16, other arithmetic, march(): return (1.0 - courant) * current + courant * upstream  22.1 us
    add x16, other arithmetic, advance(): state = decay * state + gain * plane  20.4 us
    sub x16, other arithmetic, march(): return (1.0 - courant) * current + courant * upstream  14.6 us
    dynamic_update_slice x16, other arithmetic, tile_chain(): (state, result), inflow = lax.scan(advance, (prior_state, field), filtered)  11.1 us
  transfers between devices with their start and end apart: 8, of which 7 were waited for; matrix products, arithmetic and copies ran while one was open for 2% of the time, Pallas kernels for 0%

profile of v1, /device:TPU:63, one launch (start us, length us, event | category | flops | bytes accessed | tf_op | source)
XLA Modules:
  0.0 294.0 jit_solution(15087510102781746538)
XLA Ops:
  0.6 1.9 copy-done.7
  2.5 7.2 %copy.34 = bf16[4,3,64,2048]{2,0,1,3:T(4,128)(2,1)} copy(bf16[4,3,64,2048]{3,2,1,0:T(8,128)(2,1)S(1)} %copy-done.7) | data formatting | bytes 6291456 | tf_op args[0]
  9.7 7.7 %bitcast_bitcast_fusion = bf16[2048,3,4,64]{3,2,1,0:T(4,128)(2,1)} fusion(bf16[4,3,64,2048]{2,0,1,3:T(4,128)(2,1)} %copy.34), kind=kLoop, calls=%fused_computation.90 | loop fusion | bytes 6291456
  17.4 8.7 %reshape.180 = bf16[32,2,24576]{2,1,0:T(2,128)(2,1)} reshape(bf16[2048,3,4,64]{3,2,1,0:T(4,128)(2,1)} %bitcast_bitcast_fusion) | data formatting | bytes 6291456
  26.2 7.6 %all-to-all-start = ((bf16[32,2,24576]{2,1,0:T(2,128)(2,1)}), bf16[32,2,24576]{2,1,0:T(2,128)(2,1)S(1)}, u32[]{:S(2)}, u32[]{:S(2)}) async-start(bf16[32,2,24576]{2,1,0:T(2,128)(2,1)} %reshape.180), calls=%async_computation | async-start | bytes 6291456 | tf_op jit(solution)/shard_map/all_to_all | solution.py:127
  35.2 35.0 %all-to-all-done = bf16[32,2,24576]{2,1,0:T(2,128)(2,1)S(1)} async-done(((bf16[32,2,24576]{2,1,0:T(2,128)(2,1)}), bf16[32,2,24576]{2,1,0:T(2,128)(2,1)S(1)}, u32[]{:S(2)}, u32[]{:S(2)}) %all-to-all-start) | async-done | bytes 3145760 | tf_op jit(solution)/shard_map/all_to_all | solution.py:127
  70.3 6.2 %reshape.181 = bf16[2048,3,4,64]{3,2,1,0:T(4,128)(2,1)} reshape(bf16[32,2,24576]{2,1,0:T(2,128)(2,1)S(1)} %all-to-all-done) | data formatting | bytes 6291456
  76.4 9.5 %copy.60 = bf16[4,3,32,64,64]{4,2,3,1,0:T(8,128)(2,1)} copy(bf16[4,3,32,64,64]{4,0,1,3,2:T(4,128)(2,1)} %bitcast.139) | data formatting | bytes 6291456 | tf_op jit(solution)/shard_map/all_to_all | solution.py:127
  85.9 8.5 %reshape.167 = bf16[4,3,64,4,512]{4,3,2,1,0:T(4,128)(2,1)S(1)} reshape(bf16[4,3,64,32,64]{4,3,2,1,0:T(8,128)(2,1)} %bitcast.140) | data formatting | bytes 6291456 | tf_op jit(solution)/shard_map/reshape | solution.py:13
  94.4 7.0 %constant_dynamic-slice_fusion.3 = (bf16[4,3,64,1,512]{4,3,2,1,0:T(2,128)(2,1)S(1)}, bf16[4,3,64,1,512]{4,3,2,1,0:T(2,128)(2,1)S(1)}, bf16[4,3,64,1,512]{4,3,2,1,0:T(2,128)(2,1)S(1)}, bf16[4,3,64,1,512]{4,3,2,1,0:T(2,128)(2,1)S(1)}) fusion(bf16[4,3,64,4,512]{4,3,2,1,0:T(4,128)(2,1)S(1)} %reshape.167, s32[]{:T(128)S(6)} %select_n.58, s32[]{:T(128)S(6)} %select_n.64, ...), kind=kLoop, calls=%fused_computation.80 | loop fusion | bytes 6291472 | tf_op jit(solution)/shard_map/dynamic-slice
  105.0 2.0 collective-permute-start.2
  109.7 10.6 %collective-permute-done = bf16[4,3,64,512]{3,2,1,0:T(8,128)(2,1)S(1)} collective-permute-done((bf16[4,3,64,512]{3,2,1,0:T(8,128)(2,1)S(1)}, bf16[4,3,64,512]{3,2,1,0:T(8,128)(2,1)S(1)}, u32[]{:S(2)}, u32[]{:S(2)}) %collective-permute-start) | collective-permute-done | bytes 786464 | tf_op jit(solution)/shard_map/ppermute | solution.py:29
  120.3 2.9 %collective-permute-done.1 = bf16[4,3,64,512]{3,2,1,0:T(8,128)(2,1)S(1)} collective-permute-done((bf16[4,3,64,512]{3,2,1,0:T(8,128)(2,1)S(1)}, bf16[4,3,64,512]{3,2,1,0:T(8,128)(2,1)S(1)}, u32[]{:S(2)}, u32[]{:S(2)}) %collective-permute-start.1) | collective-permute-done | bytes 786464 | tf_op jit(solution)/shard_map/ppermute | solution.py:29
  123.2 17.7 %collective-permute-done.2 = bf16[4,3,64,512]{3,2,1,0:T(8,128)(2,1)S(1)} collective-permute-done((bf16[4,3,64,512]{3,2,1,0:T(8,128)(2,1)S(1)}, bf16[4,3,64,512]{3,2,1,0:T(8,128)(2,1)S(1)}, u32[]{:S(2)}, u32[]{:S(2)}) %collective-permute-start.2) | collective-permute-done | bytes 786464 | tf_op jit(solution)/shard_map/ppermute | solution.py:29
  140.9 1.9 pad_maximum_fusion.1
  142.8 2.6 gather_fusion
  150.0 1.9 collective-permute-start.4
  151.9 3.4 %collective-permute-start.3 = (bf16[16,3,64,4]{2,0,3,1:T(8,128)(2,1)S(1)}, bf16[16,3,64,4]{2,0,3,1:T(8,128)(2,1)S(1)}, u32[]{:S(2)}, u32[]{:S(2)}) collective-permute-start(bf16[16,3,64,4]{2,0,3,1:T(8,128)(2,1)S(1)} %copy.36), channel_id=1, source_target_pairs={{0,32},{32,64},{64,96},{1,33},{33,65},{65,97},{2,34},{34,66},{66,9... | collective-permute-start | bytes 73736 | tf_op jit(solution)/shard_map/ppermute | solution.py:41
  161.1 6.0 %collective-permute-start.5 = (bf16[16,3,4,520]{3,2,1,0:T(4,128)(2,1)S(1)}, bf16[16,3,4,520]{3,2,1,0:T(4,128)(2,1)S(1)}, u32[]{:S(2)}, u32[]{:S(2)}) collective-permute-start(bf16[16,3,4,520]{3,2,1,0:T(4,128)(2,1)S(1)} %get-tuple-element.126), channel_id=1, source_target_pairs={{0,1},{1,2},{2,3},{3,4},{4,5},{5,6},{6,7},{7,8},{8,9},{9,10},{10,1... | collective-permute-start | bytes 599048 | tf_op jit(solution)/shard_map/ppermute | solution.py:41
  170.3 5.8 %collective-permute-done.6 = bf16[16,3,4,520]{3,2,1,0:T(4,128)(2,1)S(1)} collective-permute-done((bf16[16,3,4,520]{3,2,1,0:T(4,128)(2,1)S(1)}, bf16[16,3,4,520]{3,2,1,0:T(4,128)(2,1)S(1)}, u32[]{:S(2)}, u32[]{:S(2)}) %collective-permute-start.6) | collective-permute-done | bytes 199712 | tf_op jit(solution)/shard_map/ppermute | solution.py:42
  176.1 4.2 %convert_bitcast_fusion.3 = bf16[16,3,64,520]{3,2,1,0:T(8,128)(2,1)S(1)} fusion(bf16[16,3,4,520]{3,2,1,0:T(4,128)(2,1)S(1)} %collective-permute-done.6, bf16[16,3,64,4]{3,2,1,0:T(8,128)(2,1)S(1)} %copy-done.6, bf16[16,3,64,512]{3,2,1,0:T(8,128)(2,1)S(1)} %bitcast.143, bf16[16,3,64,4]{3,2,1,0:T(8,128)(2,1)S(1)} %copy-done.5, ...), kind=kOutput, calls=%fused_computation.36 | convolution fusion | flops 249600000 | bytes 6798336 | tf_op jit(solution)/shard_map/ij,pcjz->pciz/dot_general | solution.py:79
  181.2 2.6 fusion.18
  183.8 3.5 %copy.59 = f32[16,3,4,8,8,128]{5,4,2,3,1,0:T(8,128)} copy(f32[16,3,4,8,8,128]{5,4,3,2,1,0:T(8,128)S(1)} %fusion.18) | data formatting | bytes 12582912 | tf_op jit(solution)/shard_map/reshape | solution.py:73
  187.2 105.1 %while.14 = (s32[]{:T(128)}, f32[3,64,512]{2,1,0:T(8,128)S(1)}, f32[3,8,64,512]{3,2,1,0:T(8,128)S(1)}, bf16[16,3,64,512]{3,2,1,0:T(8,128)(2,1)}, f32[64,512]{1,0...) while((s32[]{:T(128)}, f32[3,64,512]{2,1,0:T(8,128)S(1)}, ...), condition=%wide.region_4.5_spmd, body=%wide.region_3.4_spmd.sunk | while | flops 4685826 | bytes 20512960 | solution.py:119
  (190 shorter events, 127.5 us)
Async XLA Ops:
  0.6 1.9 copy-start.7
  26.2 44.1 %all-to-all-start = ((bf16[32,2,24576]{2,1,0:T(2,128)(2,1)}), bf16[32,2,24576]{2,1,0:T(2,128)(2,1)S(1)}, u32[]{:S(2)}, u32[]{:S(2)}) async-start(bf16[32,2,24576]{2,1,0:T(2,128)(2,1)} %reshape.180), calls=%async_computation | async-start | bytes 6291456 | tf_op jit(solution)/shard_map/all_to_all | solution.py:127
  101.4 5.7 %copy-start.8 = (f32[6,64,512]{2,1,0:T(8,128)S(1)}, f32[6,64,512]{2,1,0:T(8,128)}, u32[]{:S(2)}) copy-start(f32[6,64,512]{2,1,0:T(8,128)} %param.10) | copy-start | bytes 2359300
  101.4 5.7 %copy-start.9 = (f32[64,512]{1,0:T(8,128)S(1)}, f32[64,512]{1,0:T(8,128)}, u32[]{:S(2)}) copy-start(f32[64,512]{1,0:T(8,128)} %param.11) | copy-start | bytes 393220
  102.1 18.2 %collective-permute-start = (bf16[4,3,64,512]{3,2,1,0:T(8,128)(2,1)S(1)}, bf16[4,3,64,512]{3,2,1,0:T(8,128)(2,1)S(1)}, u32[]{:S(2)}, u32[]{:S(2)}) collective-permute-start(bf16[4,3,64,512]{3,2,1,0:T(8,128)(2,1)S(1)} %bitcast.151), channel_id=1, source_target_pairs={{0,32},{32,64},{64,96},{96,0},{1,33},{33,65},{65,97},{97,1},{2,34}... | collective-permute-start | bytes 2359304 | tf_op jit(solution)/shard_map/ppermute | solution.py:29
  103.8 19.4 %collective-permute-start.1 = (bf16[4,3,64,512]{3,2,1,0:T(8,128)(2,1)S(1)}, bf16[4,3,64,512]{3,2,1,0:T(8,128)(2,1)S(1)}, u32[]{:S(2)}, u32[]{:S(2)}) collective-permute-start(bf16[4,3,64,512]{3,2,1,0:T(8,128)(2,1)S(1)} %bitcast.150), channel_id=1, source_target_pairs={{0,64},{32,96},{64,0},{96,32},{1,65},{33,97},{65,1},{97,33},{2,66}... | collective-permute-start | bytes 2359304 | tf_op jit(solution)/shard_map/ppermute | solution.py:29
  105.0 36.0 %collective-permute-start.2 = (bf16[4,3,64,512]{3,2,1,0:T(8,128)(2,1)S(1)}, bf16[4,3,64,512]{3,2,1,0:T(8,128)(2,1)S(1)}, u32[]{:S(2)}, u32[]{:S(2)}) collective-permute-start(bf16[4,3,64,512]{3,2,1,0:T(8,128)(2,1)S(1)} %bitcast.149), channel_id=1, source_target_pairs={{0,96},{32,0},{64,32},{96,64},{1,97},{33,1},{65,33},{97,65},{2,98}... | collective-permute-start | bytes 2359304 | tf_op jit(solution)/shard_map/ppermute | solution.py:29
  150.0 8.0 %collective-permute-start.4 = (bf16[16,3,64,4]{2,0,3,1:T(8,128)(2,1)S(1)}, bf16[16,3,64,4]{2,0,3,1:T(8,128)(2,1)S(1)}, u32[]{:S(2)}, u32[]{:S(2)}) collective-permute-start(bf16[16,3,64,4]{2,0,3,1:T(8,128)(2,1)S(1)} %copy.37), channel_id=1, source_target_pairs={{32,0},{64,32},{96,64},{33,1},{65,33},{97,65},{34,2},{66,34},{98,6... | collective-permute-start | bytes 73736 | tf_op jit(solution)/shard_map/ppermute | solution.py:42
  151.9 4.8 %collective-permute-start.3 = (bf16[16,3,64,4]{2,0,3,1:T(8,128)(2,1)S(1)}, bf16[16,3,64,4]{2,0,3,1:T(8,128)(2,1)S(1)}, u32[]{:S(2)}, u32[]{:S(2)}) collective-permute-start(bf16[16,3,64,4]{2,0,3,1:T(8,128)(2,1)S(1)} %copy.36), channel_id=1, source_target_pairs={{0,32},{32,64},{64,96},{1,33},{33,65},{65,97},{2,34},{34,66},{66,9... | collective-permute-start | bytes 73736 | tf_op jit(solution)/shard_map/ppermute | solution.py:41
  159.3 16.8 %copy-start.5 = (bf16[16,3,64,4]{3,2,1,0:T(8,128)(2,1)S(1)}, bf16[16,3,64,4]{3,2,1,0:T(8,128)(2,1)}, u32[]{:S(2)}) copy-start(bf16[16,3,64,4]{3,2,1,0:T(8,128)(2,1)} %copy.38) | copy-start | bytes 73732
  159.3 16.8 %copy-start.6 = (bf16[16,3,64,4]{3,2,1,0:T(8,128)(2,1)S(1)}, bf16[16,3,64,4]{3,2,1,0:T(8,128)(2,1)}, u32[]{:S(2)}) copy-start(bf16[16,3,64,4]{3,2,1,0:T(8,128)(2,1)} %copy.39) | copy-start | bytes 73732
  161.1 9.2 %collective-permute-start.5 = (bf16[16,3,4,520]{3,2,1,0:T(4,128)(2,1)S(1)}, bf16[16,3,4,520]{3,2,1,0:T(4,128)(2,1)S(1)}, u32[]{:S(2)}, u32[]{:S(2)}) collective-permute-start(bf16[16,3,4,520]{3,2,1,0:T(4,128)(2,1)S(1)} %get-tuple-element.126), channel_id=1, source_target_pairs={{0,1},{1,2},{2,3},{3,4},{4,5},{5,6},{6,7},{7,8},{8,9},{9,10},{10,1... | collective-permute-start | bytes 599048 | tf_op jit(solution)/shard_map/ppermute | solution.py:41
  167.1 8.9 %collective-permute-start.6 = (bf16[16,3,4,520]{3,2,1,0:T(4,128)(2,1)S(1)}, bf16[16,3,4,520]{3,2,1,0:T(4,128)(2,1)S(1)}, u32[]{:S(2)}, u32[]{:S(2)}) collective-permute-start(bf16[16,3,4,520]{3,2,1,0:T(4,128)(2,1)S(1)} %get-tuple-element.127), channel_id=1, source_target_pairs={{1,0},{2,1},{3,2},{4,3},{5,4},{6,5},{7,6},{8,7},{9,8},{10,9},{11,1... | collective-permute-start | bytes 599048 | tf_op jit(solution)/shard_map/ppermute | solution.py:42
  183.7 3.5 %copy-start.1 = (f32[3,8,64,512]{3,2,1,0:T(8,128)S(1)}, f32[3,8,64,512]{3,2,1,0:T(8,128)}, u32[]{:S(2)}) copy-start(f32[3,8,64,512]{3,2,1,0:T(8,128)} %param.15) | copy-start | bytes 9437188
  183.8 3.5 %copy-start.2 = (f32[3,64,512]{2,1,0:T(8,128)S(1)}, f32[3,64,512]{2,1,0:T(8,128)}, u32[]{:S(2)}) copy-start(f32[3,64,512]{2,1,0:T(8,128)} %param.14) | copy-start | bytes 1179652
  190.8 0.9 copy-start.3
  197.4 0.9 copy-start.3
  204.0 0.9 copy-start.3
  210.5 0.9 copy-start.3
  217.1 0.9 copy-start.3
  223.7 0.9 copy-start.3
  230.2 0.9 copy-start.3
  236.8 0.9 copy-start.3
  292.4 1.7 copy-start
  (9 other events, 7.9 us)
